TPU v7x, 256 devices: a whole 4x4x8 slice. The times are simulated.
256 devices in a mesh: sub: 4 (over y), dev: 64 (over x, z, core).
Axes of the slice: x: 4, y: 4, z: 8, core: 2. Of those that a mesh axis runs over, the one named last changes fastest.
Arguments:
- child_tiles: float32 [8192, 128, 128], P(('sub', 'dev')), parts along dimension 0, may hold values from -6 to 6
- l_slab: float32 [262144, 512], P(('sub', 'dev')), parts along dimension 0, may hold values from -6 to 6
- u_slab: float32 [512, 131072], P(None, ('sub', 'dev')), parts along dimension 1, may hold values from -0.25 to 0.25
- parent_own_entries: float32 [9216, 128, 128], P(('sub', 'dev')), parts along dimension 0, may hold values from -6 to 6
- parent_label: int32 [8, 32], P('sub'), parts along dimension 0, may hold values from 0 to 47, as said below
Outputs:
- parent_front: float32 [9216, 128, 128], P(('sub', 'dev')), parts along dimension 0
There are 4 independent parts, one for each index of `sub`. A program takes and returns all parts, laid end to end along the dimension named above; each array names one. Nothing has to cross between parts.
Inputs may be any that keep to these rules, and one draw needn't show every extreme that they name: `parent_label`: the 32 labels of one child are distinct. For child c and tile row k, the label modulo 8 is sigma((k mod 8 + k // 8 + 4 c) mod 8), with sigma a permutation of 0 to 7 common to both children.
All inputs are finite; a program needn't handle non-finite values.
Results may differ from a plain program's by a relative error of at most 0.000051.
Values sent between devices are 32-bit elements; how exact they have to be, the bound alone decides.
A program may use at most 64 MiB of HBM per device.

v0:
```python
import jax
import jax.numpy as jnp
from jax import lax
from jax.sharding import PartitionSpec as P

TILE_EDGE = 128
MT = 32
PT = 48
CGR = 4
PR = 8


def from_partner(value, axis, distance):
    mask = 2**distance
    pairs = [(source, source ^ mask) for source in range(lax.axis_size(axis))]
    return lax.ppermute(value, axis, pairs)


def tile_targets(labels, count, ndev, me_index):
    cgc = ndev // 8
    pcols = ndev // 8
    ncd = ndev // 2
    cols_loc = MT // cgc
    inner = me_index % ncd
    local = jnp.arange(count, dtype=jnp.int32)
    tile_row = inner // cgc + CGR * (local // cols_loc)
    tile_col = inner % cgc + cgc * (local % cols_loc)
    columns = jnp.arange(MT, dtype=jnp.int32)
    label_row = jnp.sum(
        jnp.where(tile_row[:, None] == columns[None, :], labels[None, :], 0), axis=1
    )
    label_col = jnp.sum(
        jnp.where(tile_col[:, None] == columns[None, :], labels[None, :], 0), axis=1
    )
    dest_dev = label_row % PR * pcols + label_col % pcols
    dest_slot = label_row // PR * (PT // pcols) + label_col // pcols
    return (dest_dev, dest_slot)


def update_tiles(child_part, left_rows, u_slab, cols_loc):
    product = jnp.dot(
        left_rows, u_slab, precision=lax.Precision.HIGHEST, preferred_element_type=jnp.float32
    )
    row_tiles = left_rows.shape[0] // TILE_EDGE
    product = (
        product.reshape(row_tiles, TILE_EDGE, cols_loc, TILE_EDGE)
        .transpose(0, 2, 1, 3)
        .reshape(row_tiles * cols_loc, TILE_EDGE, TILE_EDGE)
    )
    return child_part - product


def pack_tiles(updated, dest_dev, dest_slot, ndev, bound):
    count = updated.shape[0]
    order = jnp.arange(count, dtype=jnp.int32)
    earlier = order[None, :] < order[:, None]
    same_dest = dest_dev[:, None] == dest_dev[None, :]
    arrival = jnp.sum(jnp.where(same_dest & earlier, 1, 0), axis=1).astype(jnp.int32)
    position = dest_dev * bound + arrival
    places = jnp.arange(ndev * bound, dtype=jnp.int32)
    hits = places[:, None] == position[None, :]
    select = hits.astype(jnp.float32)
    packed = jnp.dot(
        select,
        updated.reshape(count, -1),
        precision=lax.Precision.HIGHEST,
        preferred_element_type=jnp.float32,
    )
    filled = jnp.sum(jnp.where(hits, 1, 0), axis=1)
    sent_slot = jnp.where(filled > 0, jnp.sum(jnp.where(hits, dest_slot[None, :], 0), axis=1), -1)
    return (packed.reshape(ndev, bound, -1), sent_slot.reshape(ndev, bound))


def assemble_front(incoming_tiles, incoming_slot, slot_count):
    flat = incoming_tiles.reshape(-1, incoming_tiles.shape[-1])
    select = (
        jnp.arange(slot_count, dtype=jnp.int32)[:, None] == incoming_slot.reshape(-1)[None, :]
    ).astype(jnp.float32)
    return jnp.dot(
        select, flat, precision=lax.Precision.HIGHEST, preferred_element_type=jnp.float32
    )


def body(child_tiles, l_slab, u_slab, parent_own_entries, parent_label):
    ndev = lax.axis_size("dev")
    me_index = lax.axis_index("dev")
    cgc = ndev // 8
    cols_loc = MT // cgc
    tiles_dev = child_tiles.shape[0]
    slot_count = parent_own_entries.shape[0]
    child_id = me_index // (ndev // 2)
    labels = lax.dynamic_index_in_dim(parent_label, child_id, 0, keepdims=False)
    updated = update_tiles(child_tiles, l_slab, u_slab, cols_loc)
    dest_dev, dest_slot = tile_targets(labels, tiles_dev, ndev, me_index)
    half_rows = TILE_EDGE // 2
    upper_rows = updated[:, :half_rows]
    lower_rows = updated[:, half_rows:]
    keeping = jnp.where(child_id == 0, upper_rows, lower_rows)
    giving = jnp.where(child_id == 0, lower_rows, upper_rows)
    partner_bit = (ndev // 2).bit_length() - 1
    taken = from_partner(giving, "dev", partner_bit)
    other_labels = lax.dynamic_index_in_dim(parent_label, 1 - child_id, 0, keepdims=False)
    other_dev, other_slot = tile_targets(other_labels, tiles_dev, ndev, me_index)
    pair_bound = 1
    pieces = jnp.concatenate([keeping, taken], axis=0)
    all_dev = jnp.concatenate([dest_dev, other_dev], axis=0)
    all_slot = jnp.concatenate([dest_slot, other_slot], axis=0)
    packed, sent_slot = pack_tiles(pieces, all_dev, all_slot, ndev, pair_bound)
    incoming_tiles, incoming_slot = (
        lax.all_to_all(packed, "dev", split_axis=0, concat_axis=0, tiled=True),
        lax.all_to_all(sent_slot, "dev", split_axis=0, concat_axis=0, tiled=True),
    )
    split = ndev // 2
    upper_sum = assemble_front(incoming_tiles[:split], incoming_slot[:split], slot_count).reshape(
        slot_count, half_rows, TILE_EDGE
    )
    lower_sum = assemble_front(incoming_tiles[split:], incoming_slot[split:], slot_count).reshape(
        slot_count, half_rows, TILE_EDGE
    )
    summed_entries = jnp.concatenate([upper_sum, lower_sum], axis=1)
    return parent_own_entries + summed_entries


def solution(mesh):
    in_specs = (
        P(("sub", "dev"), None, None),
        P(("sub", "dev"), None),
        P(None, ("sub", "dev")),
        P(("sub", "dev"), None, None),
        P("sub", None),
    )
    out_specs = P(("sub", "dev"), None, None)
    return jax.shard_map(body, mesh=mesh, in_specs=in_specs, out_specs=out_specs, check_vma=False)
```

profile of v0, /device:TPU:1, one launch (start us, length us, event | category | flops | bytes accessed | tf_op | source)
XLA Modules:
  0.0 119.7 jit_solution(17820394486306367219)
XLA Ops:
  0.0 0.0 copy-start
  0.0 1.6 %copy-done = f32[1024,512]{1,0:T(8,128)S(1)} copy-done((f32[1024,512]{1,0:T(8,128)S(1)}, f32[1024,512]{1,0:T(8,128)}, u32[]{:S(2)}) %copy-start) | copy-done | bytes 2097176
  1.6 6.0 %fusion.26 = f32[1024,512]{1,0:T(8,128)} fusion(f32[1024,512]{1,0:T(8,128)S(1)} %copy-done, f32[512,512]{1,0:T(8,128)} %param.7), kind=kOutput, calls=%fused_computation.79 | convolution fusion | flops 3221225472 | bytes 5242880 | tf_op jit(solution)/shard_map/dot_general | solution.py:41
  7.6 2.9 %reshape.97 = f32[8,128,4,128]{3,2,1,0:T(4,128)} reshape(f32[1024,512]{1,0:T(8,128)} %fusion.26) | data formatting | bytes 4194304 | tf_op jit(solution)/shard_map/reshape | solution.py:46
  10.5 0.0 copy-start.2
  10.5 2.0 %copy.31 = f32[8,4,128,128]{3,2,1,0:T(8,128)S(1)} copy(f32[8,4,128,128]{3,1,2,0:T(4,128)} %bitcast.44) | data formatting | bytes 4194304 | tf_op jit(solution)/shard_map/transpose | solution.py:47
  12.5 0.2 copy-done.2
  12.7 0.4 bitcast_subtract_fusion
  13.1 0.0 copy-start.3
  13.1 1.1 slice_select_fusion.1
  14.3 3.6 %collective-permute-start = (f32[32,64,128]{2,1,0:T(8,128)}, f32[32,64,128]{2,1,0:T(8,128)}, u32[]{:S(2)}, u32[]{:S(2)}) collective-permute-start(f32[32,64,128]{2,1,0:T(8,128)} %get-tuple-element.16), channel_id=1, source_target_pairs={{0,32},{1,33},{2,34},{3,35},{4,36},{5,37},{6,38},{7,39},{8,40},{9,... | collective-permute-start | bytes 3145736 | tf_op jit(solution)/shard_map/ppermute | solution.py:16
  17.8 0.0 copy-done.3
  17.9 0.2 select_reduce_fusion.5
  18.1 0.1 pad_add_fusion.1
  18.2 0.1 pad_add_fusion
  18.3 0.2 select_reduce_fusion.2
  18.4 0.1 fusion.29
  18.5 0.1 select_reduce_fusion.1
  18.7 0.7 copy.30
  19.4 10.6 %all-to-all-start = ((s32[64,1,1]{2,1,0:T(1,128)}), s32[64,1,1]{2,1,0:T(1,128)S(1)}, u32[]{:S(2)}, u32[]{:S(2)}) async-start(s32[64,1,1]{2,1,0:T(1,128)} %copy.30), calls=%async_computation | async-start | bytes 65536 | tf_op jit(solution)/shard_map/all_to_all | solution.py:111
  29.9 10.4 %collective-permute-done = f32[32,64,128]{2,1,0:T(8,128)} collective-permute-done((f32[32,64,128]{2,1,0:T(8,128)}, f32[32,64,128]{2,1,0:T(8,128)}, u32[]{:S(2)}, u32[]{:S(2)}) %collective-permute-start) | collective-permute-done | bytes 1048608 | tf_op jit(solution)/shard_map/ppermute | solution.py:16
  40.3 1.4 %pad_maximum_fusion = f32[64,64,128]{2,1,0:T(8,128)S(1)} fusion(f32[32,64,128]{2,1,0:T(8,128)} %collective-permute-done, f32[32,64,128]{2,1,0:T(8,128)S(1)} %get-tuple-element.15), kind=kLoop, calls=%fused_computation.4 | loop fusion | flops 524288 | bytes 4194304 | tf_op jit(solution)/shard_map/concatenate | solution.py:105
  41.7 2.5 %convolution_bitcast_fusion = f32[64,1,8192]{2,0,1:T(8,128)S(1)} fusion(f32[8,8,64,128]{3,2,1,0:T(8,128)S(1)} %bitcast.43, s32[64]{0:T(128)S(1)} %fusion.29), kind=kOutput, calls=%fused_computation | convolution fusion | flops 402657280 | bytes 4194560 | tf_op jit(solution)/shard_map/dot_general | solution.py:63
  44.2 3.5 %copy.32 = f32[64,1,8192]{2,1,0:T(1,128)} copy(f32[64,1,8192]{2,0,1:T(8,128)S(1)} %convolution_bitcast_fusion) | data formatting | bytes 4194304 | tf_op jit(solution)/shard_map/reshape | solution.py:71
  47.7 0.0 all-to-all-done
  47.7 14.2 %all-to-all-start.1 = ((f32[64,1,8192]{2,1,0:T(1,128)}), f32[64,1,8192]{2,1,0:T(1,128)}, u32[]{:S(2)}, u32[]{:S(2)}) async-start(f32[64,1,8192]{2,1,0:T(1,128)} %copy.32), calls=%async_computation.1 | async-start | bytes 4194304 | tf_op jit(solution)/shard_map/all_to_all | solution.py:110
  61.9 1.2 %slice_reduce_fusion.1 = (s32[32]{0:T(128)S(1)}, s32[32]{0:T(128)S(1)}) fusion(s32[64,1,1]{2,1,0:T(1,128)S(1)} %all-to-all-done), kind=kLoop, calls=%fused_computation.23 | loop fusion | bytes 512 | tf_op jit(solution)/shard_map/slice | solution.py:114
  63.1 49.9 %all-to-all-done.1 = f32[64,1,8192]{2,1,0:T(1,128)} async-done(((f32[64,1,8192]{2,1,0:T(1,128)}), f32[64,1,8192]{2,1,0:T(1,128)}, u32[]{:S(2)}, u32[]{:S(2)}) %all-to-all-start.1) | async-done | bytes 2097184 | tf_op jit(solution)/shard_map/all_to_all | solution.py:110
  113.0 1.7 %fusion.25 = (f32[32,1,8192]{2,1,0:T(1,128)S(1)}, f32[32,1,8192]{2,1,0:T(1,128)S(1)}) fusion(f32[64,1,8192]{2,1,0:T(1,128)} %all-to-all-done.1), kind=kLoop, calls=%fused_computation.78 | loop fusion | bytes 4194304 | tf_op jit(solution)/shard_map/slice | solution.py:114
  114.7 1.4 %fusion.5 = f32[36,64,128]{2,0,1:T(8,128)S(1)} fusion(s32[32]{0:T(128)S(1)} %get-tuple-element.5, f32[32,1,8192]{2,1,0:T(1,128)S(1)} %get-tuple-element.13), kind=kOutput, calls=%fused_computation.9 | convolution fusion | flops 113247360 | bytes 2228352 | tf_op jit(solution)/shard_map/dot_general | solution.py:79
  116.1 0.2 copy.35
  116.3 0.0 copy-start.1
  116.3 1.4 %fusion.2 = f32[36,64,128]{2,0,1:T(8,128)S(1)} fusion(s32[32]{0:T(128)S(1)} %get-tuple-element.6, f32[32,1,8192]{2,1,0:T(1,128)S(1)} %get-tuple-element.14), kind=kOutput, calls=%fused_computation.6 | convolution fusion | flops 113247360 | bytes 2228352 | tf_op jit(solution)/shard_map/dot_general | solution.py:79
  117.8 0.2 copy.36
  118.0 0.0 copy-done.1
  118.0 1.7 %maximum_add_fusion = f32[36,128,128]{2,1,0:T(8,128)} fusion(f32[36,128,128]{2,1,0:T(8,128)S(1)} %copy-done.1, f32[36,64,128]{2,1,0:T(8,128)S(1)} %copy.36, f32[36,64,128]{2,1,0:T(8,128)S(1)} %copy.35), kind=kLoop, calls=%fused_computation.1 | loop fusion | flops 1179648 | bytes 7077888 | tf_op jit(solution)/shard_map/add | solution.py:121
  (5 shorter events, 0.0 us)
Async XLA Ops:
  0.0 1.6 %copy-start = (f32[1024,512]{1,0:T(8,128)S(1)}, f32[1024,512]{1,0:T(8,128)}, u32[]{:S(2)}) copy-start(f32[1024,512]{1,0:T(8,128)} %param.6) | copy-start | bytes 6291460
  10.5 2.2 %copy-start.2 = (f32[32,128,128]{2,1,0:T(8,128)S(1)}, f32[32,128,128]{2,1,0:T(8,128)}, u32[]{:S(2)}) copy-start(f32[32,128,128]{2,1,0:T(8,128)} %param.5) | copy-start | bytes 6291460
  13.1 4.7 %copy-start.3 = (s32[2,32]{1,0:T(2,128)S(1)}, s32[2,32]{1,0:T(2,128)}, u32[]{:S(2)}) copy-start(s32[2,32]{1,0:T(2,128)} %param.9) | copy-start | bytes 772
  14.3 26.0 %collective-permute-start = (f32[32,64,128]{2,1,0:T(8,128)}, f32[32,64,128]{2,1,0:T(8,128)}, u32[]{:S(2)}, u32[]{:S(2)}) collective-permute-start(f32[32,64,128]{2,1,0:T(8,128)} %get-tuple-element.16), channel_id=1, source_target_pairs={{0,32},{1,33},{2,34},{3,35},{4,36},{5,37},{6,38},{7,39},{8,40},{9,... | collective-permute-start | bytes 3145736 | tf_op jit(solution)/shard_map/ppermute | solution.py:16
  19.4 28.3 %all-to-all-start = ((s32[64,1,1]{2,1,0:T(1,128)}), s32[64,1,1]{2,1,0:T(1,128)S(1)}, u32[]{:S(2)}, u32[]{:S(2)}) async-start(s32[64,1,1]{2,1,0:T(1,128)} %copy.30), calls=%async_computation | async-start | bytes 65536 | tf_op jit(solution)/shard_map/all_to_all | solution.py:111
  47.7 65.3 %all-to-all-start.1 = ((f32[64,1,8192]{2,1,0:T(1,128)}), f32[64,1,8192]{2,1,0:T(1,128)}, u32[]{:S(2)}, u32[]{:S(2)}) async-start(f32[64,1,8192]{2,1,0:T(1,128)} %copy.32), calls=%async_computation.1 | async-start | bytes 4194304 | tf_op jit(solution)/shard_map/all_to_all | solution.py:110
  116.3 1.7 %copy-start.1 = (f32[36,128,128]{2,1,0:T(8,128)S(1)}, f32[36,128,128]{2,1,0:T(8,128)}, u32[]{:S(2)}) copy-start(f32[36,128,128]{2,1,0:T(8,128)} %param.8) | copy-start | bytes 7077892
where the time goes:
time: 120 us
  waiting for transfers between devices  60.3 us (50%)
  starting transfers between devices  28.3 us (24%)
  local copies, waits for them, and re-layouts  14.3 us (12%)
  matrix products  11.3 us (9%)
  other arithmetic  5.36 us (4%)
    all_to_all x1, waiting for transfers between devices, body(): lax.all_to_all(packed, 'dev', split_axis=0, concat_axis=0, tiled=True)  49.9 us
    all_to_all x1, starting transfers between devices, body(): lax.all_to_all(packed, 'dev', split_axis=0, concat_axis=0, tiled=True)  14.2 us
    all_to_all x1, starting transfers between devices, body(): lax.all_to_all(sent_slot, 'dev', split_axis=0, concat_axis=0, tiled=True)  10.6 us
    ppermute x1, waiting for transfers between devices, from_partner(): return lax.ppermute(value, axis, pairs)  10.4 us
    dot_general x1, matrix products, update_tiles(): jnp.dot(left_rows, u_slab, precision=lax.Precision.HIGHEST, preferred_ele...  5.97 us
    ppermute x1, starting transfers between devices, from_partner(): return lax.ppermute(value, axis, pairs)  3.57 us
    reshape x1, local copies, waits for them, and re-layouts, pack_tiles(): return (packed.reshape(ndev, bound, -1), sent_slot.reshape(ndev, bound))  3.49 us
    reshape x1, local copies, waits for them, and re-layouts, update_tiles(): product.reshape(row_tiles, TILE_EDGE, cols_loc, TILE_EDGE)  2.95 us
  transfers between devices with their start and end apart: 3, of which 2 were waited for; matrix products, arithmetic and copies ran while one was open for 8% of the time, Pallas kernels for 0%

commit v1 on v0

v1 whole, which is shorter than its diff:
```python
import functools

import jax
import jax.numpy as jnp
from jax import lax
from jax.experimental import pallas as pl
from jax.experimental.pallas import tpu as pltpu
from jax.sharding import PartitionSpec as P

TILE = 128
F32 = jnp.float32
BF16 = jnp.bfloat16
MESH = pl.DeviceIdType.MESH
CHUNKS = ((0, 8), (8, 16), (24, 32), (56, 32), (88, 40))
NCH = len(CHUNKS)
OWNERS = 32
ZERO = OWNERS


def place(index):
    return index // 16, index // 2 % 8, index % 2


def offset(order):
    group = order // 4
    size = 4 - (group + 1) // 2
    step = size * (2 * (group % 2) - 1)
    return order // 2 % 2, step, order % 2


def owner(me, order):
    x, z, core = place(me)
    flip_x, step, flip_core = offset(order)
    to_x = x // 2 * 2 + (x + flip_x) % 2
    to_z = (z + step + 8) % 8
    to_core = (core + flip_core) % 2
    return to_x, to_z, to_core


def kernel(labels_hbm, child_hbm, l_hbm, u_hbm, entries_hbm, front, *scratch):
    (child, left, right, right_hi, right_lo, outgoing, packed) = scratch[:7]
    swapped = scratch[7 : 7 + NCH]
    received = scratch[7 + NCH : 7 + 2 * NCH]
    own = scratch[7 + 2 * NCH : 7 + 3 * NCH]
    labels, row_at, own_at, other_at, load_sem, swap_send, swap_recv, send_sem, recv_sem = (
        scratch[7 + 3 * NCH :]
    )
    me = lax.axis_index("dev")
    x, z, core = place(me)
    side = x // 2
    partner = me + (3 - 2 * x) * 16
    my_slot = x % 2 * 16 + z * 2 + core
    row_class = x % 2 * 2 + z // 4
    col_class = z % 4 * 2 + core

    loads = [
        pltpu.make_async_copy(source, target, load_sem.at[n])
        for n, (source, target) in enumerate(
            ((u_hbm, right), (l_hbm, left), (child_hbm, child), (entries_hbm, front), (labels_hbm, labels))
        )
    ]
    loads[4].start()
    for load in loads[:3]:
        load.start()

    barrier = pltpu.get_barrier_semaphore()
    pl.semaphore_signal(barrier, inc=1, device_id={"dev": partner}, device_id_type=MESH)

    def greet(order):
        to_x, to_z, to_core = owner(me, order)
        pl.semaphore_signal(
            barrier,
            inc=1,
            device_id={"dev": to_x * 16 + to_z * 2 + to_core},
            device_id_type=MESH,
        )

    def greet_step(order, carry):
        greet(order)
        return carry

    lax.fori_loop(0, 28, greet_step, 0)
    for order in (29, 30, 31):
        greet(order)

    loads[4].wait()
    row_classes = [labels[side, row_class + 4 * k] % 8 for k in range(8)]
    for c in range(8):
        at = jnp.int32(0)
        for k in range(1, 8):
            at = jnp.where(row_classes[k] == c, k, at)
        row_at[c] = at
    own_classes = [labels[side, col_class + 8 * m] % 8 for m in range(4)]
    other_classes = [labels[1 - side, col_class + 8 * m] % 8 for m in range(4)]
    for c in range(8):
        at = jnp.int32(-1)
        for m in range(4):
            at = jnp.where(own_classes[m] == c, m, at)
        own_at[c] = at
        at = jnp.int32(0)
        for m in range(1, 4):
            at = jnp.where(other_classes[m] == c, m, at)
        other_at[c] = at

    loads[0].wait()
    right_hi[...] = right[...].astype(BF16)
    right_lo[...] = (right[...] - right_hi[...].astype(F32)).astype(BF16)
    loads[1].wait()
    loads[2].wait()

    def update(c, put):
        k = row_at[c]
        rows = left[k]
        high = rows.astype(BF16)
        low = (rows - high.astype(F32)).astype(BF16)
        for half in range(2):
            columns = pl.ds(half * 256, 256)
            hi_columns = right_hi[:, columns]
            product = jnp.dot(high, hi_columns, preferred_element_type=F32)
            product += jnp.dot(low, hi_columns, preferred_element_type=F32)
            product += jnp.dot(high, right_lo[:, columns], preferred_element_type=F32)
            for part in range(2):
                m = 2 * half + part
                put(m, child[k * 4 + m] - product[:, part * TILE : part * TILE + TILE])

    def other_step(n, carry):
        def put(m, tile):
            outgoing[n * 4 + m] = tile

        update((1 - side) * 4 + n, put)
        return carry

    def own_step(n, carry):
        def put(m, tile):
            for part, (first, count) in zip(own, CHUNKS):
                part[n * 4 + m] = tile[first : first + count]

        update(side * 4 + n, put)
        return carry

    lax.fori_loop(0, 4, other_step, 0)
    pl.semaphore_wait(barrier, OWNERS)

    swaps = []
    for n, (first, count) in enumerate(CHUNKS):
        swaps.append(
            pltpu.make_async_remote_copy(
                src_ref=outgoing.at[:, pl.ds(first, count), :],
                dst_ref=swapped[n],
                send_sem=swap_send.at[n],
                recv_sem=swap_recv.at[n],
                device_id={"dev": partner},
                device_id_type=MESH,
            )
        )
        swaps[n].start()
    loads[3].start()
    lax.fori_loop(0, 4, own_step, 0)

    for n, (first, count) in enumerate(CHUNKS):
        rows = pl.ds(first, count)
        received[n][ZERO] = jnp.zeros((count, TILE), F32)
        swaps[n].wait_recv()

        def pick(order, n=n):
            to_x, to_z, to_core = owner(me, order)
            base = (to_x % 2 * 2 + to_z // 4) * 4
            c = to_z % 4 * 2 + to_core
            mine = own_at[c]
            here = own[n][base + jnp.maximum(mine, 0)]
            there = swapped[n][base + other_at[c]]
            return jnp.where(mine >= 0, here, there)

        def pack(order, rows=rows, pick=pick):
            packed[order, rows, :] = pick(order)

        def send(order, n=n, rows=rows):
            to_x, to_z, to_core = owner(me, order)
            pltpu.make_async_remote_copy(
                src_ref=packed.at[order, rows, :],
                dst_ref=received[n].at[my_slot],
                send_sem=send_sem.at[n],
                recv_sem=recv_sem.at[n],
                device_id={"dev": to_x * 16 + to_z * 2 + to_core},
                device_id_type=MESH,
            ).start()

        def step(order, carry, pack=pack, send=send):
            pack(order + 1)
            send(order)
            return carry

        pack(0)
        lax.fori_loop(0, 27, step, 0)
        pack(29)
        send(27)
        pack(30)
        send(29)
        pack(31)
        send(30)
        received[n][my_slot] = pick(28)
        send(31)

    row_mine = x * 2 + z // 4
    col_mine = z % 4 * 2 + core
    row_part = [[], []]
    col_part = [[], []]
    for c in range(2):
        for s in range(6):
            at = jnp.int32(-1)
            for i in range(32):
                x_part = jnp.where(side == c, i % 4 // 2, 1 - i % 4 // 2)
                at = jnp.where(
                    labels[c, i] == 8 * s + row_mine, x_part * 16 + i % 2 * 8, at
                )
            row_part[c].append(at)
            at = jnp.int32(-1)
            for j in range(32):
                at = jnp.where(labels[c, j] == 8 * s + col_mine, j % 8, at)
            col_part[c].append(at)

    loads[3].wait()
    for n, (first, count) in enumerate(CHUNKS):
        rows = pl.ds(first, count)
        arrived = received[n].at[pl.ds(0, OWNERS - 1)]
        pltpu.make_async_copy(arrived, arrived, recv_sem.at[n]).wait()
        for slot in range(36):
            total = front[slot, rows, :]
            for c in range(2):
                r, q = row_part[c][slot // 6], col_part[c][slot % 6]
                at = jnp.where((r >= 0) & (q >= 0), r + q, ZERO)
                total += received[n][at]
            front[slot, rows, :] = total
    for n, (first, count) in enumerate(CHUNKS):
        swaps[n].wait_send()
        sent = packed.at[pl.ds(0, OWNERS - 1), pl.ds(first, count), :]
        pltpu.make_async_copy(sent, sent, send_sem.at[n]).wait()


def body(child_tiles, l_slab, u_slab, parent_own_entries, parent_label):
    far = pl.BlockSpec(memory_space=pltpu.HBM)
    dma = pltpu.SemaphoreType.DMA
    return pl.pallas_call(
        kernel,
        name="extend_add",
        out_shape=pltpu.VMEM(parent_own_entries.shape, F32),
        in_specs=[far] * 5,
        out_specs=pl.BlockSpec(memory_space=pltpu.VMEM),
        scratch_shapes=[
            pltpu.VMEM((32, TILE, TILE), F32),
            pltpu.VMEM((8, TILE, 512), F32),
            pltpu.VMEM((512, 512), F32),
            pltpu.VMEM((512, 512), BF16),
            pltpu.VMEM((512, 512), BF16),
            pltpu.VMEM((16, TILE, TILE), F32),
            pltpu.VMEM((OWNERS, TILE, TILE), F32),
            *[pltpu.VMEM((16, count, TILE), F32) for _, count in CHUNKS],
            *[pltpu.VMEM((OWNERS + 1, count, TILE), F32) for _, count in CHUNKS],
            *[pltpu.VMEM((16, count, TILE), F32) for _, count in CHUNKS],
            pltpu.SMEM((2, 32), jnp.int32),
            pltpu.SMEM((8,), jnp.int32),
            pltpu.SMEM((8,), jnp.int32),
            pltpu.SMEM((8,), jnp.int32),
            dma((5,)),
            dma((NCH,)),
            dma((NCH,)),
            dma((NCH,)),
            dma((NCH,)),
        ],
        compiler_params=pltpu.CompilerParams(
            collective_id=0, has_side_effects=True, vmem_limit_bytes=40 * 2**20
        ),
    )(
        *[
            pltpu.with_memory_space_constraint(array, pltpu.HBM)
            for array in (
                parent_label,
                child_tiles,
                l_slab.reshape(8, TILE, 512),
                u_slab,
                parent_own_entries,
            )
        ]
    )


def solution(mesh):
    in_specs = (
        P(("sub", "dev"), None, None),
        P(("sub", "dev"), None),
        P(None, ("sub", "dev")),
        P(("sub", "dev"), None, None),
        P("sub", None),
    )
    out_specs = P(("sub", "dev"), None, None)
    return jax.shard_map(body, mesh=mesh, in_specs=in_specs, out_specs=out_specs, check_vma=False)
```

time: 120 us -> 63.5 us (0.53)
  Pallas kernels: 0 us -> 62 us
  waiting for transfers between devices: 60.3 us -> 0 us
  starting transfers between devices: 28.3 us -> 0 us
  local copies, waits for them, and re-layouts: 14.3 us -> 1.41 us
  matrix products: 11.3 us -> 0 us
  other arithmetic: 5.36 us -> 0 us
    pallas_call x0 -> x1, Pallas kernels: none -> 62 us  [body(): pl.pallas_call(kernel, name='extend_add', out_shape=pltpu.VMEM(parent_own...]
    all_to_all x2 -> x0, waiting for transfers between devices: 49.9 us -> none  [the longest x1 49.9 us: body(): lax.all_to_all(packed, 'dev', split_axis=0, concat_axis=0, tiled=True)]
    all_to_all x2 -> x0, starting transfers between devices: 24.7 us -> none  [the longest x1 14.2 us: body(): lax.all_to_all(packed, 'dev', split_axis=0, concat_axis=0, tiled=True)]
    dot_general x4 -> x0, matrix products: 11.3 us -> none  [the longest x1 5.97 us: update_tiles(): jnp.dot(left_rows, u_slab, precision=lax.Precision.HIGHEST, preferred_ele...]
    ppermute x1 -> x0, waiting for transfers between devices: 10.4 us -> none  [from_partner(): return lax.ppermute(value, axis, pairs)]
    reshape x2 -> x0, local copies, waits for them, and re-layouts: 6.44 us -> none  [the longest x1 3.49 us: pack_tiles(): return (packed.reshape(ndev, bound, -1), sent_slot.reshape(ndev, bound))]
    ppermute x1 -> x0, starting transfers between devices: 3.57 us -> none  [from_partner(): return lax.ppermute(value, axis, pairs)]
    slice x2 -> x0, local copies, waits for them, and re-layouts: 2.91 us -> none  [the longest x1 1.68 us: body(): incoming_tiles[:split]]
  transfers between devices with their start and end apart: 3 -> 0, of which waited for: 2 -> 0; matrix products, arithmetic and copies ran while one was open for 8% -> 0% of each run, Pallas kernels for 0% -> 0%
where the time goes in v1:
time: 63.5 us; the launch traced here: 63.4 us
  Pallas kernels  62 us (98%)
  local copies, waits for them, and re-layouts  1.41 us (2%)
    pallas_call x1, Pallas kernels, body(): pl.pallas_call(kernel, name='extend_add', out_shape=pltpu.VMEM(parent_own...  62 us
    unnamed x1, local copies, waits for them, and re-layouts  1.41 us

profile of v1, /device:TPU:1, one launch (start us, length us, event | category | flops | bytes accessed | tf_op | source)
XLA Modules:
  0.0 63.4 jit_solution(11556274774805169543)
XLA Ops:
  0.0 62.0 %extend_add.1 = f32[36,128,128]{2,1,0:T(8,128)S(1)} custom-call(s32[2,32]{1,0:T(2,128)} %labels_hbm.1, f32[32,128,128]{2,1,0:T(8,128)} %child_hbm.1, f32[8,128,512]{2,1,0:T(8,128)} %bitcast.1, f32[512,512]{1,0:T(8,128)} %u_hbm.1, f32[36,128,128]{2,1,0:T(8,128)} %entries_hbm.1), custom_call_target="tpu_custom_call" | custom-call | tf_op jit(solution)/shard_map/extend_add/pallas_call | solution.py:243
  62.0 1.4 %copy.7 = f32[36,128,128]{2,1,0:T(8,128)} copy(f32[36,128,128]{2,1,0:T(8,128)S(1)} %extend_add.1) | data formatting | bytes 4718592

commit v2 on v1

v2 whole, which is shorter than its diff:
```python
import jax
import jax.numpy as jnp
from jax import lax
from jax.experimental import pallas as pl
from jax.experimental.pallas import tpu as pltpu
from jax.sharding import PartitionSpec as P

TILE = 128
F32 = jnp.float32
BF16 = jnp.bfloat16
MESH = pl.DeviceIdType.MESH
CHUNKS = ((0, 8), (8, 8), (16, 16), (32, 24), (56, 32), (88, 40))
NCH = len(CHUNKS)
FIRST = 16
EARLY = 2
OWNERS = 32
ZERO = OWNERS


def split(value):
    high = value.astype(BF16)
    return high, (value - high.astype(F32)).astype(BF16)


def kernel(labels_hbm, child_hbm, l_hbm, u_hbm, entries_hbm, front, *scratch):
    (child, child_first, left, left_first, right, right_hi, right_lo) = scratch[:7]
    outgoing_first, outgoing, packed = scratch[7:10]
    received = scratch[10 : 10 + NCH]
    own = scratch[10 + NCH : 10 + 2 * NCH]
    swapped = scratch[10 + 2 * NCH : 10 + 4 * NCH]
    labels, row_at, own_at, other_at, load_sem, swap_send, swap_recv, send_sem, recv_sem = (
        scratch[10 + 4 * NCH :]
    )
    me = lax.axis_index("dev")
    x, z, core = lax.div(me, 16), lax.rem(lax.div(me, 2), 8), lax.rem(me, 2)
    side, x_low, z_high = lax.div(x, 2), lax.rem(x, 2), lax.div(z, 4)
    partner = me + (3 - 2 * x) * 16
    my_slot = x_low * 16 + z * 2 + core
    row_class = x_low * 2 + z_high
    col_class = lax.rem(z, 4) * 2 + core

    loads = [
        pltpu.make_async_copy(source, target, load_sem.at[n])
        for n, (source, target) in enumerate(
            (
                (labels_hbm, labels),
                (u_hbm, right),
                (l_hbm.at[:, pl.ds(0, FIRST), :], left_first),
                (child_hbm.at[:, pl.ds(0, FIRST), :], child_first),
                (l_hbm, left),
                (child_hbm, child),
                (entries_hbm, front),
            )
        )
    ]
    for load in loads[:4]:
        load.start()

    flips = [(fx, fc) for fx in range(2) for fc in range(2)]
    to_core = [core, 1 - core]
    to_x_low = [x_low, 1 - x_low]
    base = [(side * 2 + to_x_low[fx]) * 16 + to_core[fc] for fx, fc in flips]

    barrier = pltpu.get_barrier_semaphore()

    def greet(device):
        pl.semaphore_signal(barrier, inc=1, device_id={"dev": device}, device_id_type=MESH)

    for step in (3, 5, 4, 2, 6, 1, 7):
        for n in range(4):
            greet(base[n] + lax.rem(z + step, 8) * 2)
        if step == 5:
            greet(partner)
    for n in (1, 2, 3):
        greet(base[n] + z * 2)
    for load in loads[4:6]:
        load.start()

    loads[0].wait()
    row_classes = [lax.rem(labels[side, row_class + 4 * k], 8) for k in range(8)]
    for c in range(8):
        at = jnp.int32(0)
        for k in range(1, 8):
            at = jnp.where(row_classes[k] == c, k, at)
        row_at[c] = at
    own_classes = [lax.rem(labels[side, col_class + 8 * m], 8) for m in range(4)]
    other_classes = [lax.rem(labels[1 - side, col_class + 8 * m], 8) for m in range(4)]
    for c in range(8):
        at = jnp.int32(-1)
        for m in range(4):
            at = jnp.where(own_classes[m] == c, m, at)
        own_at[c] = at
        at = jnp.int32(0)
        for m in range(1, 4):
            at = jnp.where(other_classes[m] == c, m, at)
        other_at[c] = at

    loads[1].wait()
    right_hi[...], right_lo[...] = split(right[...])
    loads[2].wait()
    loads[3].wait()

    def multiply(rows, columns):
        high, low = split(rows)
        hi_columns = right_hi[:, columns]
        product = jnp.dot(high, hi_columns, preferred_element_type=F32)
        product += jnp.dot(low, hi_columns, preferred_element_type=F32)
        return product + jnp.dot(high, right_lo[:, columns], preferred_element_type=F32)

    classes = [n % 2 * 2 + n // 2 for n in range(4)]
    at = [row_at[(1 - side) * 4 + c] for c in classes] + [row_at[side * 4 + c] for c in classes]
    rows = jnp.concatenate([left_first[k] for k in at], axis=0)
    for half in range(2):
        product = multiply(rows, pl.ds(half * 256, 256))
        for n, k in enumerate(at):
            for part in range(2):
                m = 2 * half + part
                tile = product[n * FIRST : (n + 1) * FIRST, part * TILE : (part + 1) * TILE]
                tile = child_first[k * 4 + m] - tile
                if n < 4:
                    outgoing_first[n * 4 + m] = tile
                else:
                    for first, count in CHUNKS[:EARLY]:
                        own[0 if first == 0 else 1][(n - 4) * 4 + m] = tile[first : first + count]
    pl.semaphore_wait(barrier, OWNERS)

    swaps = []
    for n, (first, count) in enumerate(CHUNKS):
        source = outgoing_first if n < EARLY else outgoing
        for half in range(2):
            tiles = pl.ds(half * 8, 8)
            swaps.append(
                pltpu.make_async_remote_copy(
                    src_ref=source.at[tiles, pl.ds(first, count), :],
                    dst_ref=swapped[2 * n + half],
                    send_sem=swap_send.at[2 * n + half],
                    recv_sem=swap_recv.at[2 * n + half],
                    device_id={"dev": partner},
                    device_id_type=MESH,
                )
            )
    for swap in swaps[: 2 * EARLY]:
        swap.start()

    loads[4].wait()
    loads[5].wait()

    def update(c, put):
        ks = [row_at[c], row_at[c + 2]]
        rows = jnp.concatenate([left[k] for k in ks], axis=0)
        for half in range(2):
            product = multiply(rows, pl.ds(half * 256, 256))
            for n, k in enumerate(ks):
                for part in range(2):
                    m = 2 * half + part
                    tile = product[n * TILE : (n + 1) * TILE, part * TILE : (part + 1) * TILE]
                    put(n, m, child[k * 4 + m] - tile)

    def other_step(pair, carry):
        def put(n, m, tile):
            outgoing[(pair * 2 + n) * 4 + m] = tile

        update((1 - side) * 4 + pair, put)
        return carry

    def own_step(pair, carry):
        def put(n, m, tile):
            for part, (first, count) in list(zip(own, CHUNKS))[EARLY:]:
                part[(pair * 2 + n) * 4 + m] = tile[first : first + count]

        update(side * 4 + pair, put)
        return carry

    lax.fori_loop(0, 2, other_step, 0)
    for swap in swaps[2 * EARLY :]:
        swap.start()
    loads[6].start()
    for n, (first, count) in enumerate(CHUNKS):
        rows = pl.ds(first, count)
        received[n][ZERO] = jnp.zeros((count, TILE), F32)
        if n == 1:
            lax.fori_loop(0, 2, own_step, 0)

        def send(to_z, n=n, rows=rows):
            for i in range(4):

                def start(i=i):
                    pltpu.make_async_remote_copy(
                        src_ref=packed.at[to_z * 4 + i, rows, :],
                        dst_ref=received[n].at[my_slot],
                        send_sem=send_sem.at[n],
                        recv_sem=recv_sem.at[n],
                        device_id={"dev": base[i] + to_z * 2},
                        device_id_type=MESH,
                    ).start()

                if i:
                    start()
                else:
                    pl.when(to_z != z)(start)

        for half in range(2):
            first_z, way = (0, 1) if half == 0 else (7, -1)

            def pick(to_z, fx, fc, n=n, half=half):
                c = lax.rem(to_z, 4) * 2 + to_core[fc]
                mine, other = own_at[c], other_at[c]
                place = to_x_low[fx] * 4
                here = own[n][half * 8 + place + jnp.maximum(mine, 0)]
                there = swapped[2 * n + half][place + other]
                return jnp.where(mine >= 0, here, there)

            def pack(to_z, rows=rows, pick=pick):
                for i, (fx, fc) in enumerate(flips):
                    packed[to_z * 4 + i, rows, :] = pick(to_z, fx, fc)

            def step(q, carry, pack=pack, send=send, first_z=first_z, way=way):
                pack(first_z + way * (q + 1))
                send(first_z + way * q)
                return carry

            swaps[2 * n + half].wait_recv()
            pack(jnp.int32(first_z))
            lax.fori_loop(0, 3, step, 0)

            def keep(n=n, pick=pick):
                received[n][my_slot] = pick(z, 0, 0)

            pl.when(z_high == half)(keep)
            send(jnp.int32(first_z + 3 * way))

    row_part = [[], []]
    col_part = [[], []]
    for c in range(2):
        for s in range(6):
            at = jnp.int32(-1)
            for i in range(32):
                x_part = jnp.where(side == c, i % 4 // 2, 1 - i % 4 // 2)
                here = labels[c, i] == 8 * s + x * 2 + z_high
                at = jnp.where(here, x_part * 16 + i % 2 * 8, at)
            row_part[c].append(at)
            at = jnp.int32(-1)
            for j in range(32):
                at = jnp.where(labels[c, j] == 8 * s + col_class, j % 8, at)
            col_part[c].append(at)

    loads[6].wait()
    for n, (first, count) in enumerate(CHUNKS):
        rows = pl.ds(first, count)
        arrived = received[n].at[pl.ds(0, OWNERS - 1)]
        pltpu.make_async_copy(arrived, arrived, recv_sem.at[n]).wait()
        for slot in range(36):
            total = front[slot, rows, :]
            for c in range(2):
                r, q = row_part[c][slot // 6], col_part[c][slot % 6]
                total += received[n][jnp.where((r >= 0) & (q >= 0), r + q, ZERO)]
            front[slot, rows, :] = total
    for swap in swaps:
        swap.wait_send()
    for n, (first, count) in enumerate(CHUNKS):
        sent = packed.at[pl.ds(0, OWNERS - 1), pl.ds(first, count), :]
        pltpu.make_async_copy(sent, sent, send_sem.at[n]).wait()


def body(child_tiles, l_slab, u_slab, parent_own_entries, parent_label):
    far = pl.BlockSpec(memory_space=pltpu.HBM)
    dma = pltpu.SemaphoreType.DMA
    return pl.pallas_call(
        kernel,
        name="extend_add",
        out_shape=pltpu.VMEM(parent_own_entries.shape, F32),
        in_specs=[far] * 5,
        out_specs=pl.BlockSpec(memory_space=pltpu.VMEM),
        scratch_shapes=[
            pltpu.VMEM((32, TILE, TILE), F32),
            pltpu.VMEM((32, FIRST, TILE), F32),
            pltpu.VMEM((8, TILE, 512), F32),
            pltpu.VMEM((8, FIRST, 512), F32),
            pltpu.VMEM((512, 512), F32),
            pltpu.VMEM((512, 512), BF16),
            pltpu.VMEM((512, 512), BF16),
            pltpu.VMEM((16, FIRST, TILE), F32),
            pltpu.VMEM((16, TILE, TILE), F32),
            pltpu.VMEM((OWNERS, TILE, TILE), F32),
            *[pltpu.VMEM((OWNERS + 1, count, TILE), F32) for _, count in CHUNKS],
            *[pltpu.VMEM((16, count, TILE), F32) for _, count in CHUNKS],
            *[pltpu.VMEM((8, count, TILE), F32) for _, count in CHUNKS for _ in range(2)],
            pltpu.SMEM((2, 32), jnp.int32),
            pltpu.SMEM((8,), jnp.int32),
            pltpu.SMEM((8,), jnp.int32),
            pltpu.SMEM((8,), jnp.int32),
            dma((7,)),
            dma((2 * NCH,)),
            dma((2 * NCH,)),
            dma((NCH,)),
            dma((NCH,)),
        ],
        compiler_params=pltpu.CompilerParams(
            collective_id=0, has_side_effects=True, vmem_limit_bytes=40 * 2**20
        ),
    )(
        *[
            pltpu.with_memory_space_constraint(array, pltpu.HBM)
            for array in (
                parent_label,
                child_tiles,
                l_slab.reshape(8, TILE, 512),
                u_slab,
                parent_own_entries,
            )
        ]
    )


def solution(mesh):
    in_specs = (
        P(("sub", "dev"), None, None),
        P(("sub", "dev"), None),
        P(None, ("sub", "dev")),
        P(("sub", "dev"), None, None),
        P("sub", None),
    )
    out_specs = P(("sub", "dev"), None, None)
    return jax.shard_map(body, mesh=mesh, in_specs=in_specs, out_specs=out_specs, check_vma=False)
```

time: 63.5 us -> 59.4 us (0.935)
  the two profiles are of different devices: /device:TPU:1 before, /device:TPU:67 now
where the time goes in v2:
time: 59.4 us; the launch traced here: 59.2 us
  Pallas kernels  57.8 us (97%)
  local copies, waits for them, and re-layouts  1.41 us (2%)
    pallas_call x1, Pallas kernels, body(): pl.pallas_call(kernel, name='extend_add', out_shape=pltpu.VMEM(parent_own...  57.8 us
    unnamed x1, local copies, waits for them, and re-layouts  1.41 us

profile of v2, /device:TPU:67, one launch (start us, length us, event | category | flops | bytes accessed | tf_op | source)
XLA Modules:
  0.0 59.2 jit_solution(16736669631199095402)
XLA Ops:
  0.0 57.8 %extend_add.1 = f32[36,128,128]{2,1,0:T(8,128)S(1)} custom-call(s32[2,32]{1,0:T(2,128)} %labels_hbm.1, f32[32,128,128]{2,1,0:T(8,128)} %child_hbm.1, f32[8,128,512]{2,1,0:T(8,128)} %bitcast.1, f32[512,512]{1,0:T(8,128)} %u_hbm.1, f32[36,128,128]{2,1,0:T(8,128)} %entries_hbm.1), custom_call_target="tpu_custom_call" | custom-call | tf_op jit(solution)/shard_map/extend_add/pallas_call | solution.py:268
  57.8 1.4 %copy.7 = f32[36,128,128]{2,1,0:T(8,128)} copy(f32[36,128,128]{2,1,0:T(8,128)S(1)} %extend_add.1) | data formatting | bytes 4718592

commit v3 on v2

--- a/solution.py
+++ b/solution.py
@@ -9,10 +9,12 @@
 F32 = jnp.float32
 BF16 = jnp.bfloat16
 MESH = pl.DeviceIdType.MESH
-CHUNKS = ((0, 8), (8, 8), (16, 16), (32, 24), (56, 32), (88, 40))
+CHUNKS = ((0, 8), (8, 8), (16, 24), (40, 40), (80, 48))
 NCH = len(CHUNKS)
 FIRST = 16
 EARLY = 2
+APART = 1
+ORDERS = (((0, 1, 2, 3), (7, 6, 5, 4)),) * NCH
 OWNERS = 32
 ZERO = OWNERS
 
@@ -27,10 +29,9 @@
     outgoing_first, outgoing, packed = scratch[7:10]
     received = scratch[10 : 10 + NCH]
     own = scratch[10 + NCH : 10 + 2 * NCH]
-    swapped = scratch[10 + 2 * NCH : 10 + 4 * NCH]
-    labels, row_at, own_at, other_at, load_sem, swap_send, swap_recv, send_sem, recv_sem = (
-        scratch[10 + 4 * NCH :]
-    )
+    swapped = scratch[10 + 2 * NCH : 10 + 6 * NCH]
+    labels, row_at, own_at, other_at, load_sem, known_sem = scratch[10 + 6 * NCH :][:6]
+    swap_send, swap_recv, send_sem, recv_sem = scratch[10 + 6 * NCH :][6:]
     me = lax.axis_index("dev")
     x, z, core = lax.div(me, 16), lax.rem(lax.div(me, 2), 8), lax.rem(me, 2)
     side, x_low, z_high = lax.div(x, 2), lax.rem(x, 2), lax.div(z, 4)
@@ -56,23 +57,29 @@
     for load in loads[:4]:
         load.start()
 
-    flips = [(fx, fc) for fx in range(2) for fc in range(2)]
     to_core = [core, 1 - core]
-    to_x_low = [x_low, 1 - x_low]
-    base = [(side * 2 + to_x_low[fx]) * 16 + to_core[fc] for fx, fc in flips]
+    base = [[(side * 2 + xl) * 16 + to_core[fc] for fc in range(2)] for xl in range(2)]
 
     barrier = pltpu.get_barrier_semaphore()
 
-    def greet(device):
-        pl.semaphore_signal(barrier, inc=1, device_id={"dev": device}, device_id_type=MESH)
-
-    for step in (3, 5, 4, 2, 6, 1, 7):
-        for n in range(4):
-            greet(base[n] + lax.rem(z + step, 8) * 2)
-        if step == 5:
-            greet(partner)
-    for n in (1, 2, 3):
-        greet(base[n] + z * 2)
+    def signal(semaphore, device):
+        pl.semaphore_signal(semaphore, inc=1, device_id={"dev": device}, device_id_type=MESH)
+
+    def along(step):
+        return lax.rem(z + step + 8, 8) * 2
+
+    mine = (side * 2 + x_low) * 16 + core
+    others = [
+        (side * 2 + x_low) * 16 + 1 - core,
+        (side * 2 + 1 - x_low) * 16 + core,
+        (side * 2 + 1 - x_low) * 16 + 1 - core,
+    ]
+    for step in (1, -1):
+        for column in others[::-1] + [mine]:
+            signal(barrier, column + along(step))
+    signal(barrier, partner)
+    for column in others:
+        signal(barrier, column + z * 2)
     for load in loads[4:6]:
         load.start()
 
@@ -122,28 +129,33 @@
                 else:
                     for first, count in CHUNKS[:EARLY]:
                         own[0 if first == 0 else 1][(n - 4) * 4 + m] = tile[first : first + count]
-    pl.semaphore_wait(barrier, OWNERS)
+    pl.semaphore_wait(barrier, 12)
 
     swaps = []
     for n, (first, count) in enumerate(CHUNKS):
         source = outgoing_first if n < EARLY else outgoing
-        for half in range(2):
-            tiles = pl.ds(half * 8, 8)
+        for piece in range(4):
+            tiles = pl.ds(piece * 4, 4)
             swaps.append(
                 pltpu.make_async_remote_copy(
                     src_ref=source.at[tiles, pl.ds(first, count), :],
-                    dst_ref=swapped[2 * n + half],
-                    send_sem=swap_send.at[2 * n + half],
-                    recv_sem=swap_recv.at[2 * n + half],
+                    dst_ref=swapped[4 * n + piece],
+                    send_sem=swap_send.at[4 * n + piece],
+                    recv_sem=swap_recv.at[4 * n + piece],
                     device_id={"dev": partner},
                     device_id_type=MESH,
                 )
             )
-    for swap in swaps[: 2 * EARLY]:
+    for swap in swaps[: 4 * EARLY]:
         swap.start()
+    for step in (1, -1):
+        signal(known_sem.at[0], mine + along(step))
 
     loads[4].wait()
     loads[5].wait()
+    pl.semaphore_wait(known_sem.at[0], 2)
+    for step in (2, -2):
+        signal(known_sem.at[1], mine + along(step))
 
     def update(c, put):
         ks = [row_at[c], row_at[c + 2]]
@@ -172,62 +184,66 @@
         return carry
 
     lax.fori_loop(0, 2, other_step, 0)
-    for swap in swaps[2 * EARLY :]:
+    for swap in swaps[4 * EARLY :]:
         swap.start()
     loads[6].start()
+    pl.semaphore_wait(known_sem.at[1], 2)
+
     for n, (first, count) in enumerate(CHUNKS):
         rows = pl.ds(first, count)
         received[n][ZERO] = jnp.zeros((count, TILE), F32)
         if n == 1:
             lax.fori_loop(0, 2, own_step, 0)
 
-        def send(to_z, n=n, rows=rows):
-            for i in range(4):
-
-                def start(i=i):
-                    pltpu.make_async_remote_copy(
-                        src_ref=packed.at[to_z * 4 + i, rows, :],
-                        dst_ref=received[n].at[my_slot],
-                        send_sem=send_sem.at[n],
-                        recv_sem=recv_sem.at[n],
-                        device_id={"dev": base[i] + to_z * 2},
-                        device_id_type=MESH,
-                    ).start()
-
-                if i:
-                    start()
-                else:
-                    pl.when(to_z != z)(start)
-
-        for half in range(2):
-            first_z, way = (0, 1) if half == 0 else (7, -1)
-
-            def pick(to_z, fx, fc, n=n, half=half):
+        for pieces in ((0,), (1,), (2,), (3,)) if n < APART else ((0, 1), (2, 3)):
+            half = pieces[0] // 2
+            order = ORDERS[n][half]
+
+            def pick(to_z, fc, piece, n=n):
                 c = lax.rem(to_z, 4) * 2 + to_core[fc]
                 mine, other = own_at[c], other_at[c]
-                place = to_x_low[fx] * 4
-                here = own[n][half * 8 + place + jnp.maximum(mine, 0)]
-                there = swapped[2 * n + half][place + other]
+                here = own[n][piece * 4 + jnp.maximum(mine, 0)]
+                there = swapped[4 * n + piece][other]
                 return jnp.where(mine >= 0, here, there)
 
-            def pack(to_z, rows=rows, pick=pick):
-                for i, (fx, fc) in enumerate(flips):
-                    packed[to_z * 4 + i, rows, :] = pick(to_z, fx, fc)
-
-            def step(q, carry, pack=pack, send=send, first_z=first_z, way=way):
-                pack(first_z + way * (q + 1))
-                send(first_z + way * q)
-                return carry
-
-            swaps[2 * n + half].wait_recv()
-            pack(jnp.int32(first_z))
-            lax.fori_loop(0, 3, step, 0)
-
-            def keep(n=n, pick=pick):
-                received[n][my_slot] = pick(z, 0, 0)
-
-            pl.when(z_high == half)(keep)
-            send(jnp.int32(first_z + 3 * way))
+            def pack(to_z, rows=rows, pick=pick, pieces=pieces):
+                for piece in pieces:
+                    for fc in range(2):
+                        packed[to_z * 4 + piece % 2 * 2 + fc, rows, :] = pick(to_z, fc, piece)
+
+            def send(to_z, n=n, rows=rows, pieces=pieces):
+                for piece in pieces:
+                    xl = piece % 2
+                    for fc in range(2):
+
+                        def start(fc=fc, xl=xl):
+                            pltpu.make_async_remote_copy(
+                                src_ref=packed.at[to_z * 4 + xl * 2 + fc, rows, :],
+                                dst_ref=received[n].at[my_slot],
+                                send_sem=send_sem.at[n],
+                                recv_sem=recv_sem.at[n],
+                                device_id={"dev": base[xl][fc] + to_z * 2},
+                                device_id_type=MESH,
+                            ).start()
+
+                        if fc:
+                            start()
+                        else:
+                            pl.when((to_z != z) | (x_low != xl))(start)
+
+            for piece in pieces:
+                swaps[4 * n + piece].wait_recv()
+            pack(order[0])
+            for to_z, next_z in zip(order, order[1:]):
+                pack(next_z)
+                send(to_z)
+            for piece in pieces:
+
+                def keep(n=n, pick=pick, piece=piece):
+                    received[n][my_slot] = pick(z, 0, piece)
+
+                pl.when((z_high == half) & (x_low == piece % 2))(keep)
+            send(order[-1])
 
     row_part = [[], []]
     col_part = [[], []]
@@ -284,14 +300,15 @@
             pltpu.VMEM((OWNERS, TILE, TILE), F32),
             *[pltpu.VMEM((OWNERS + 1, count, TILE), F32) for _, count in CHUNKS],
             *[pltpu.VMEM((16, count, TILE), F32) for _, count in CHUNKS],
-            *[pltpu.VMEM((8, count, TILE), F32) for _, count in CHUNKS for _ in range(2)],
+            *[pltpu.VMEM((4, count, TILE), F32) for _, count in CHUNKS for _ in range(4)],
             pltpu.SMEM((2, 32), jnp.int32),
             pltpu.SMEM((8,), jnp.int32),
             pltpu.SMEM((8,), jnp.int32),
             pltpu.SMEM((8,), jnp.int32),
             dma((7,)),
-            dma((2 * NCH,)),
-            dma((2 * NCH,)),
+            pltpu.SemaphoreType.REGULAR((2,)),
+            dma((4 * NCH,)),
+            dma((4 * NCH,)),
             dma((NCH,)),
             dma((NCH,)),
         ],

time: 59.4 us -> 58.6 us (0.987)
  Pallas kernels: 57.8 us -> 57.1 us
    pallas_call x1, Pallas kernels: 57.8 us -> 57.1 us  [body(): pl.pallas_call(kernel, name='extend_add', out_shape=pltpu.VMEM(parent_own...]
where the time goes in v3:
time: 58.6 us; the launch traced here: 58.5 us
  Pallas kernels  57.1 us (97%)
  local copies, waits for them, and re-layouts  1.41 us (2%)
    pallas_call x1, Pallas kernels, body(): pl.pallas_call(kernel, name='extend_add', out_shape=pltpu.VMEM(parent_own...  57.1 us
    unnamed x1, local copies, waits for them, and re-layouts  1.41 us

profile of v3, /device:TPU:67, one launch (start us, length us, event | category | flops | bytes accessed | tf_op | source)
XLA Modules:
  0.0 58.5 jit_solution(7217102196891543447)
XLA Ops:
  0.0 57.1 %extend_add.1 = f32[36,128,128]{2,1,0:T(8,128)S(1)} custom-call(s32[2,32]{1,0:T(2,128)} %labels_hbm.1, f32[32,128,128]{2,1,0:T(8,128)} %child_hbm.1, f32[8,128,512]{2,1,0:T(8,128)} %bitcast.1, f32[512,512]{1,0:T(8,128)} %u_hbm.1, f32[36,128,128]{2,1,0:T(8,128)} %entries_hbm.1), custom_call_target="tpu_custom_call" | custom-call | tf_op jit(solution)/shard_map/extend_add/pallas_call | solution.py:284
  57.1 1.4 %copy.7 = f32[36,128,128]{2,1,0:T(8,128)} copy(f32[36,128,128]{2,1,0:T(8,128)S(1)} %extend_add.1) | data formatting | bytes 4718592

commit v4 on v3

--- a/solution.py
+++ b/solution.py
@@ -9,11 +9,12 @@
 F32 = jnp.float32
 BF16 = jnp.bfloat16
 MESH = pl.DeviceIdType.MESH
-CHUNKS = ((0, 8), (8, 8), (16, 24), (40, 40), (80, 48))
+CHUNKS = ((0, 8), (8, 8), (16, 16), (32, 40), (72, 56))
 NCH = len(CHUNKS)
 FIRST = 16
 EARLY = 2
 APART = 1
+RELAY, FROM, VIA, TO = 2, 6, 3, 2
 ORDERS = (((0, 1, 2, 3), (7, 6, 5, 4)),) * NCH
 OWNERS = 32
 ZERO = OWNERS
@@ -25,6 +26,8 @@
 
 
 def kernel(labels_hbm, child_hbm, l_hbm, u_hbm, entries_hbm, front, *scratch):
+    passing, pass_sem = scratch[-2:]
+    scratch = scratch[:-2]
     (child, child_first, left, left_first, right, right_hi, right_lo) = scratch[:7]
     outgoing_first, outgoing, packed = scratch[7:10]
     received = scratch[10 : 10 + NCH]
@@ -211,7 +214,7 @@
                     for fc in range(2):
                         packed[to_z * 4 + piece % 2 * 2 + fc, rows, :] = pick(to_z, fc, piece)
 
-            def send(to_z, n=n, rows=rows, pieces=pieces):
+            def send_direct(to_z, n=n, rows=rows, pieces=pieces):
                 for piece in pieces:
                     xl = piece % 2
                     for fc in range(2):
@@ -231,6 +234,23 @@
                         else:
                             pl.when((to_z != z) | (x_low != xl))(start)
 
+            def send_indirect(rows=rows, n=n):
+                pltpu.make_async_remote_copy(
+                    src_ref=packed.at[pl.ds(TO * 4, 4), rows, :],
+                    dst_ref=passing,
+                    send_sem=send_sem.at[n],
+                    recv_sem=pass_sem.at[0],
+                    device_id={"dev": mine + VIA * 2},
+                    device_id_type=MESH,
+                ).start()
+
+            def send(to_z, n=n, direct=send_direct, indirect=send_indirect):
+                if n == RELAY and to_z == TO:
+                    pl.when(z == FROM)(indirect)
+                    pl.when(z != FROM)(lambda: direct(to_z))
+                else:
+                    direct(to_z)
+
             for piece in pieces:
                 swaps[4 * n + piece].wait_recv()
             pack(order[0])
@@ -244,6 +264,23 @@
 
                 pl.when((z_high == half) & (x_low == piece % 2))(keep)
             send(order[-1])
+
+        if n == RELAY + 1:
+
+            def forward():
+                pltpu.make_async_copy(passing, passing, pass_sem.at[0]).wait()
+                for xl in range(2):
+                    for fc in range(2):
+                        pltpu.make_async_remote_copy(
+                            src_ref=passing.at[xl * 2 + fc],
+                            dst_ref=received[RELAY].at[x_low * 16 + FROM * 2 + core],
+                            send_sem=pass_sem.at[1],
+                            recv_sem=recv_sem.at[RELAY],
+                            device_id={"dev": base[xl][fc] + TO * 2},
+                            device_id_type=MESH,
+                        ).start()
+
+            pl.when(z == VIA)(forward)
 
     row_part = [[], []]
     col_part = [[], []]
@@ -271,6 +308,7 @@
                 r, q = row_part[c][slot // 6], col_part[c][slot % 6]
                 total += received[n][jnp.where((r >= 0) & (q >= 0), r + q, ZERO)]
             front[slot, rows, :] = total
+    pl.when(z == VIA)(lambda: pltpu.make_async_copy(passing, passing, pass_sem.at[1]).wait())
     for swap in swaps:
         swap.wait_send()
     for n, (first, count) in enumerate(CHUNKS):
@@ -311,6 +349,8 @@
             dma((4 * NCH,)),
             dma((NCH,)),
             dma((NCH,)),
+            pltpu.VMEM((4, CHUNKS[RELAY][1], TILE), F32),
+            dma((2,)),
         ],
         compiler_params=pltpu.CompilerParams(
             collective_id=0, has_side_effects=True, vmem_limit_bytes=40 * 2**20

time: 58.6 us -> 57.9 us (0.988)
  Pallas kernels: 57.1 us -> 56.4 us
    pallas_call x1, Pallas kernels: 57.1 us -> 56.4 us  [body(): pl.pallas_call(kernel, name='extend_add', out_shape=pltpu.VMEM(parent_own...]
where the time goes in v4:
time: 57.9 us; the launch traced here: 57.8 us
  Pallas kernels  56.4 us (97%)
  local copies, waits for them, and re-layouts  1.41 us (2%)
    pallas_call x1, Pallas kernels, body(): pl.pallas_call(kernel, name='extend_add', out_shape=pltpu.VMEM(parent_own...  56.4 us
    unnamed x1, local copies, waits for them, and re-layouts  1.41 us

profile of v4, /device:TPU:67, one launch (start us, length us, event | category | flops | bytes accessed | tf_op | source)
XLA Modules:
  0.0 57.8 jit_solution(11119297572185698730)
XLA Ops:
  0.0 56.4 %extend_add.1 = f32[36,128,128]{2,1,0:T(8,128)S(1)} custom-call(s32[2,32]{1,0:T(2,128)} %labels_hbm.1, f32[32,128,128]{2,1,0:T(8,128)} %child_hbm.1, f32[8,128,512]{2,1,0:T(8,128)} %bitcast.1, f32[512,512]{1,0:T(8,128)} %u_hbm.1, f32[36,128,128]{2,1,0:T(8,128)} %entries_hbm.1), custom_call_target="tpu_custom_call" | custom-call | tf_op jit(solution)/shard_map/extend_add/pallas_call | solution.py:322
  56.4 1.4 %copy.7 = f32[36,128,128]{2,1,0:T(8,128)} copy(f32[36,128,128]{2,1,0:T(8,128)S(1)} %extend_add.1) | data formatting | bytes 4718592

commit v5 on v4

--- a/solution.py
+++ b/solution.py
@@ -14,7 +14,8 @@
 FIRST = 16
 EARLY = 2
 APART = 1
-RELAY, FROM, VIA, TO = 2, 6, 3, 2
+RELAY = 2
+DETOURS = ((6, 3, 2), (3, 6, 7))
 ORDERS = (((0, 1, 2, 3), (7, 6, 5, 4)),) * NCH
 OWNERS = 32
 ZERO = OWNERS
@@ -234,20 +235,22 @@
                         else:
                             pl.when((to_z != z) | (x_low != xl))(start)
 
-            def send_indirect(rows=rows, n=n):
+            def send_indirect(to_z, via, rows=rows, n=n):
                 pltpu.make_async_remote_copy(
-                    src_ref=packed.at[pl.ds(TO * 4, 4), rows, :],
+                    src_ref=packed.at[pl.ds(to_z * 4, 4), rows, :],
                     dst_ref=passing,
                     send_sem=send_sem.at[n],
                     recv_sem=pass_sem.at[0],
-                    device_id={"dev": mine + VIA * 2},
+                    device_id={"dev": mine + via * 2},
                     device_id_type=MESH,
                 ).start()
 
             def send(to_z, n=n, direct=send_direct, indirect=send_indirect):
-                if n == RELAY and to_z == TO:
-                    pl.when(z == FROM)(indirect)
-                    pl.when(z != FROM)(lambda: direct(to_z))
+                detour = [d for d in DETOURS if d[2] == to_z] if n == RELAY else []
+                if detour:
+                    from_z, via, _ = detour[0]
+                    pl.when(z == from_z)(lambda: indirect(to_z, via))
+                    pl.when(z != from_z)(lambda: direct(to_z))
                 else:
                     direct(to_z)
 
@@ -267,20 +270,21 @@
 
         if n == RELAY + 1:
 
-            def forward():
+            def forward(from_z, to_z):
                 pltpu.make_async_copy(passing, passing, pass_sem.at[0]).wait()
                 for xl in range(2):
                     for fc in range(2):
                         pltpu.make_async_remote_copy(
                             src_ref=passing.at[xl * 2 + fc],
-                            dst_ref=received[RELAY].at[x_low * 16 + FROM * 2 + core],
+                            dst_ref=received[RELAY].at[x_low * 16 + from_z * 2 + core],
                             send_sem=pass_sem.at[1],
                             recv_sem=recv_sem.at[RELAY],
-                            device_id={"dev": base[xl][fc] + TO * 2},
+                            device_id={"dev": base[xl][fc] + to_z * 2},
                             device_id_type=MESH,
                         ).start()
 
-            pl.when(z == VIA)(forward)
+            for from_z, via, to_z in DETOURS:
+                pl.when(z == via)(lambda from_z=from_z, to_z=to_z: forward(from_z, to_z))
 
     row_part = [[], []]
     col_part = [[], []]
@@ -308,7 +312,8 @@
                 r, q = row_part[c][slot // 6], col_part[c][slot % 6]
                 total += received[n][jnp.where((r >= 0) & (q >= 0), r + q, ZERO)]
             front[slot, rows, :] = total
-    pl.when(z == VIA)(lambda: pltpu.make_async_copy(passing, passing, pass_sem.at[1]).wait())
+    for _, via, _ in DETOURS:
+        pl.when(z == via)(lambda: pltpu.make_async_copy(passing, passing, pass_sem.at[1]).wait())
     for swap in swaps:
         swap.wait_send()
     for n, (first, count) in enumerate(CHUNKS):

time: 57.9 us -> 58 us (level)
  no operation moved by 1% of the time
where the time goes in v5:
time: 58 us; the launch traced here: 57.9 us
  Pallas kernels  56.5 us (97%)
  local copies, waits for them, and re-layouts  1.41 us (2%)
    pallas_call x1, Pallas kernels, body(): pl.pallas_call(kernel, name='extend_add', out_shape=pltpu.VMEM(parent_own...  56.5 us
    unnamed x1, local copies, waits for them, and re-layouts  1.41 us

profile of v5, /device:TPU:67, one launch (start us, length us, event | category | flops | bytes accessed | tf_op | source)
XLA Modules:
  0.0 57.9 jit_solution(6692988987994353152)
XLA Ops:
  0.0 56.5 %extend_add.1 = f32[36,128,128]{2,1,0:T(8,128)S(1)} custom-call(s32[2,32]{1,0:T(2,128)} %labels_hbm.1, f32[32,128,128]{2,1,0:T(8,128)} %child_hbm.1, f32[8,128,512]{2,1,0:T(8,128)} %bitcast.1, f32[512,512]{1,0:T(8,128)} %u_hbm.1, f32[36,128,128]{2,1,0:T(8,128)} %entries_hbm.1), custom_call_target="tpu_custom_call" | custom-call | tf_op jit(solution)/shard_map/extend_add/pallas_call | solution.py:327
  56.5 1.4 %copy.7 = f32[36,128,128]{2,1,0:T(8,128)} copy(f32[36,128,128]{2,1,0:T(8,128)S(1)} %extend_add.1) | data formatting | bytes 4718592
